TPU v7x, 32 devices: a whole 2x2x4 slice. The times are simulated.
32 devices in a mesh: rep: 2 (over core), ep: 16 (over z, y, x).
Axes of the slice: x: 2, y: 2, z: 4, core: 2. Of those that a mesh axis runs over, the one named last changes fastest.
Arguments:
- tokens: bfloat16 [4096, 2048], P(('rep', 'ep')), may hold values from -6 to 6
- gates: float32 [4096], P(('rep', 'ep')), may hold values from 0.25 to 1
- expert_ids: int32 [4096, 1], P(('rep', 'ep')), may hold values from 0 to 3; in each aligned block of 128 rows (0 to 127, 128 to 255, ...) at most 40 rows name the same one
- weight_in: bfloat16 [2048, 16384], P(None, 'ep'), may hold values from -0.125 to 0.125
- weight_out: bfloat16 [16384, 2048], P('ep'), may hold values from -0.09375 to 0.09375
Outputs:
- mixed: bfloat16 [4096, 2048], P(('rep', 'ep'))
Inputs may be any that keep to these rules, and one draw needn't show every extreme that they name: `expert_ids`: among the 128 rows of one device no expert is named by more than 40 rows, and some expert is named by exactly that many in some devices' rows; every expert is named somewhere.
All inputs are finite; a program needn't handle non-finite values.
Results may differ from a plain program's by a relative error of at most 0.0057.
Values may be sent and summed in bfloat16 or wider, within the bound.
A program may use at most 64 MiB of HBM per device.

v0:
```python
import functools

import jax
import jax.numpy as jnp
from jax import lax
from jax.experimental import pallas as pl
from jax.experimental.pallas import tpu as pltpu
from jax.sharding import PartitionSpec as P

SLICES = 4
CHUNKS = 4
STEP = 512
ORDER = "a1b0a2b1c0a3b2c1d1b3c2d2e1c3d3e2d0f1e3f2e0f3f0"
BF16 = jnp.bfloat16
F32 = jnp.float32
MESH = pl.DeviceIdType.MESH


def layout(owner_count, tok_rows):
    groups = owner_count // SLICES
    chunks = CHUNKS
    per = groups // chunks
    seats = 3 * tok_rows // (4 * groups) + tok_rows // (2 * groups)
    unit = 8 if per == 1 else 16
    seats = -(-seats // unit) * unit
    offsets = [0]
    for far in range(1, groups // 2 + 1):
        offsets += [far, groups - far]
    return groups, chunks, per, seats, offsets[:groups]


def stack_rows(blocks):
    return jnp.concatenate([block.astype(F32) for block in blocks], axis=0).astype(BF16)


def kernel(
    owner_count,
    ids_row,
    gates,
    tokens,
    weight_in,
    weight_out,
    out,
    w_in,
    w_out,
    send,
    gathered,
    staged,
    hidden,
    parts,
    diag_a,
    diag_b,
    from_x,
    from_y,
    sums,
    returned,
    w_sem,
    z_send,
    z_recv,
    g_send,
    g_recv,
    r_send,
    r_recv,
    b_send,
    b_recv,
):
    tok_rows, width = tokens.shape
    groups, chunks, per, seats, offsets = layout(owner_count, tok_rows)
    half = width // 2
    me = lax.axis_index("ep")
    group = me // SLICES
    lane = me % SLICES
    x_bit, y_bit = lane % 2, lane // 2
    x_lane = y_bit * 2 + (1 - x_bit)
    y_lane = (1 - y_bit) * 2 + x_bit
    d_lane = (1 - y_bit) * 2 + (1 - x_bit)
    x_dev = group * SLICES + x_lane
    y_dev = group * SLICES + y_lane

    load_in = pltpu.make_async_copy(weight_in, w_in, w_sem.at[0])
    load_out = pltpu.make_async_copy(weight_out, w_out, w_sem.at[1])
    load_in.start()
    load_out.start()

    barrier = pltpu.get_barrier_semaphore()
    pl.semaphore_signal(barrier, inc=1, device_id={"ep": x_dev}, device_id_type=MESH)
    pl.semaphore_signal(barrier, inc=1, device_id={"ep": y_dev}, device_id_type=MESH)
    for off in range(1, groups):
        other = (group + off) % groups * SLICES + lane
        pl.semaphore_signal(barrier, inc=1, device_id={"ep": other}, device_id_type=MESH)

    lanes_e = -(-groups // 16) * 16
    t0 = lax.broadcasted_iota(jnp.int32, (tok_rows, tok_rows), 0)
    t1 = lax.broadcasted_iota(jnp.int32, (tok_rows, tok_rows), 1)
    ids = ids_row[...]
    hot = (lax.broadcasted_iota(jnp.int32, (lanes_e, tok_rows), 0) == ids).astype(F32)
    ahead = jnp.dot(hot.astype(BF16), (t0 < t1).astype(F32).astype(BF16), preferred_element_type=F32)
    slot = ids * seats + jnp.sum(hot * ahead, axis=0, keepdims=True).astype(jnp.int32)

    def take(target, dst):
        seat = lax.broadcasted_iota(jnp.int32, (seats, tok_rows), 0) + target * seats
        place = (seat == slot).astype(F32).astype(BF16)
        for c in range(0, width, STEP):
            rows = jnp.dot(place, tokens[:, c : c + STEP], preferred_element_type=F32)
            dst[:, c : c + STEP] = rows.astype(BF16)

    def remote(src, dst, s_sem, r_sem, dev):
        return pltpu.make_async_remote_copy(
            src_ref=src,
            dst_ref=dst,
            send_sem=s_sem,
            recv_sem=r_sem,
            device_id={"ep": dev},
            device_id_type=MESH,
        )

    def seat_block(ref, k):
        return ref.at[pl.ds(k % per * seats, seats)] if per > 1 else ref

    spread, forward, diag, pair, z_copies, back = {}, {}, {}, {}, {}, {}

    def take_for(k):
        target = (group - offsets[k] + groups) % groups
        take(target, send.at[k])
        z_copies[k] = remote(
            send.at[k],
            seat_block(gathered.at[k // per, lane], k),
            z_send.at[k],
            z_recv.at[k],
            target * SLICES + lane,
        )

    def stage_a(j):
        for k in range(j * per, (j + 1) * per):
            if k > 0:
                z_copies[k].wait_recv()
        own = gathered.at[j, lane]
        spread[j] = [
            remote(own, own, g_send.at[j, 0], g_recv.at[j, 0], x_dev),
            remote(own, own, g_send.at[j, 1], g_recv.at[j, 1], y_dev),
        ]
        for copy in spread[j]:
            copy.start()

    def stage_b(j):
        first = gathered.at[j, x_lane, :, pl.ds(0, half)]
        second = gathered.at[j, y_lane, :, pl.ds(half, half)]
        forward[j] = [
            remote(first, first, g_send.at[j, 2], g_recv.at[j, 2], y_dev),
            remote(second, second, g_send.at[j, 3], g_recv.at[j, 3], x_dev),
        ]
        for arrived, onward in zip(spread[j], forward[j]):
            arrived.wait_recv()
            onward.start()

    def stage_c(j):
        for copy in forward[j]:
            copy.wait_recv()
        staged[...] = stack_rows([gathered[j, s] for s in range(SLICES)])
        if j == 0:
            load_in.wait()
        tile = STEP
        rows = staged.shape[0] // SLICES

        @pl.loop(0, w_in.shape[1] // tile)
        def _(n):
            cols = pl.ds(pl.multiple_of(n * tile, tile), tile)
            value = jnp.dot(staged[...], w_in[:, cols], preferred_element_type=F32)
            hidden[:, cols] = jnp.maximum(value, 0.0).astype(BF16)

        if j == 0:
            load_out.wait()

        @pl.loop(0, width // tile)
        def _(n):
            cols = pl.ds(pl.multiple_of(n * tile, tile), tile)
            value = jnp.dot(hidden[...], w_out[:, cols], preferred_element_type=F32)
            for s in range(SLICES):
                parts[j, s, :, cols] = value[s * rows : (s + 1) * rows].astype(BF16)

    def stage_d(j):
        diag[j] = [
            remote(
                parts.at[j, d_lane, :, pl.ds(0, half)],
                diag_a.at[j],
                r_send.at[j, 0],
                r_recv.at[j, 0],
                y_dev,
            ),
            remote(
                parts.at[j, d_lane, :, pl.ds(half, half)],
                diag_b.at[j],
                r_send.at[j, 1],
                r_recv.at[j, 1],
                x_dev,
            ),
        ]
        for copy in diag[j]:
            copy.start()

    def stage_e(j):
        pair[j] = [
            remote(parts.at[j, x_lane], from_x.at[j], r_send.at[j, 2], r_recv.at[j, 2], x_dev),
            remote(parts.at[j, y_lane], from_y.at[j], r_send.at[j, 3], r_recv.at[j, 3], y_dev),
        ]
        diag[j][0].wait_recv()
        parts[j, x_lane, :, :half] = (
            parts[j, x_lane, :, :half].astype(F32) + diag_a[j].astype(F32)
        ).astype(BF16)
        pair[j][0].start()
        diag[j][1].wait_recv()
        parts[j, y_lane, :, half:] = (
            parts[j, y_lane, :, half:].astype(F32) + diag_b[j].astype(F32)
        ).astype(BF16)
        pair[j][1].start()

    def stage_f(j):
        for copy in pair[j]:
            copy.wait_recv()
        sums[j] = (
            parts[j, lane].astype(F32) + from_x[j].astype(F32) + from_y[j].astype(F32)
        ).astype(BF16)
        for k in range(j * per, (j + 1) * per):
            if k > 0:
                source = (group + offsets[k]) % groups
                src = seat_block(sums.at[j], k)
                back[k] = remote(
                    src, returned.at[k], b_send.at[k], b_recv.at[k], source * SLICES + lane
                )
                back[k].start()

    take(group, seat_block(gathered.at[0, lane], 0))
    take_for(1)
    pl.semaphore_wait(barrier, 2 + groups - 1)
    if per == 1:
        stage_a(0)
    for k in range(2, groups):
        take_for(k)
        z_copies[k - 1].start()
    z_copies[groups - 1].start()
    if per > 1:
        stage_a(0)

    stages = {"a": stage_a, "b": stage_b, "c": stage_c, "d": stage_d, "e": stage_e, "f": stage_f}
    for name, j in zip(ORDER[::2], ORDER[1::2]):
        stages[name](int(j))

    slot_c = jnp.sum(jnp.where(t0 == t1, slot, 0), axis=1, keepdims=True)
    weight = jnp.sum(jnp.where(t0 == t1, gates[...], 0.0), axis=1, keepdims=True)
    picks = []
    for k in range(groups):
        if k > 0:
            back[k].wait_recv()
        target = (group - offsets[k] + groups) % groups
        seat = lax.broadcasted_iota(jnp.int32, (tok_rows, seats), 1) + target * seats
        picks.append((seat == slot_c).astype(F32))
    pick = jnp.concatenate(picks, axis=1).astype(BF16)
    for c in range(0, width, STEP):
        blocks = [sums[0, :seats, c : c + STEP]]
        blocks += [returned[k, :, c : c + STEP] for k in range(1, groups)]
        picked = jnp.dot(pick, stack_rows(blocks), preferred_element_type=F32)
        out[:, c : c + STEP] = (weight * picked).astype(BF16)

    for j in range(chunks):
        for copy in spread[j] + forward[j] + diag[j] + pair[j]:
            copy.wait_send()
    for k in range(1, groups):
        z_copies[k].wait_send()
        back[k].wait_send()


def body(tokens, gates, expert_ids, weight_in, weight_out):
    owner_count = lax.axis_size("ep")
    tok_rows, width = tokens.shape
    groups, chunks, per, seats, _ = layout(owner_count, tok_rows)
    rows = per * seats
    half = width // 2
    vmem = pl.BlockSpec(memory_space=pltpu.VMEM)
    hbm = pl.BlockSpec(memory_space=pl.ANY)
    dma = pltpu.SemaphoreType.DMA
    return pl.pallas_call(
        functools.partial(kernel, owner_count),
        out_shape=jax.ShapeDtypeStruct((tok_rows, width), BF16),
        in_specs=[vmem] * 3 + [hbm] * 2,
        out_specs=vmem,
        scratch_shapes=[
            pltpu.VMEM(weight_in.shape, BF16),
            pltpu.VMEM(weight_out.shape, BF16),
            pltpu.VMEM((groups, seats, width), BF16),
            pltpu.VMEM((chunks, SLICES, rows, width), BF16),
            pltpu.VMEM((SLICES * rows, width), BF16),
            pltpu.VMEM((SLICES * rows, weight_in.shape[1]), BF16),
            pltpu.VMEM((chunks, SLICES, rows, width), BF16),
            pltpu.VMEM((chunks, rows, half), BF16),
            pltpu.VMEM((chunks, rows, half), BF16),
            pltpu.VMEM((chunks, rows, width), BF16),
            pltpu.VMEM((chunks, rows, width), BF16),
            pltpu.VMEM((chunks, rows, width), BF16),
            pltpu.VMEM((groups, seats, width), BF16),
            dma((2,)),
            dma((groups,)),
            dma((groups,)),
            dma((chunks, 4)),
            dma((chunks, 4)),
            dma((chunks, 4)),
            dma((chunks, 4)),
            dma((groups,)),
            dma((groups,)),
        ],
        compiler_params=pltpu.CompilerParams(
            collective_id=0, has_side_effects=True, vmem_limit_bytes=60 * 1024 * 1024
        ),
    )(
        expert_ids.reshape(1, tok_rows),
        gates.reshape(1, tok_rows),
        tokens,
        weight_in,
        weight_out,
    )


def solution(mesh):
    in_specs = (
        P(("rep", "ep"), None),
        P(("rep", "ep")),
        P(("rep", "ep"), None),
        P(None, "ep"),
        P("ep", None),
    )
    out_specs = P(("rep", "ep"), None)
    return jax.shard_map(body, mesh=mesh, in_specs=in_specs, out_specs=out_specs, check_vma=False)
```

profile of v0, /device:TPU:0, one launch (start us, length us, event | category | flops | bytes accessed | tf_op | source)
XLA Modules:
  0.0 58.9 jit_solution(14032560193628394321)
XLA Ops:
  0.0 57.0 %shard_map.55 = bf16[128,2048]{1,0:T(8,128)(2,1)} custom-call(s32[1,128]{1,0:T(1,128)} %bitcast.2, f32[1,128]{1,0:T(1,128)} %bitcast.3, bf16[128,2048]{1,0:T(8,128)(2,1)} %tokens.1, bf16[2048,1024]{1,0:T(8,128)(2,1)} %weight_in.1, bf16[1024,2048]{1,0:T(8,128)(2,1)} %weight_out.1), custom_call_target="tpu_custom_call" | custom-call | tf_op jit(solution)/shard_map/pallas_call | solution.py:281
  57.0 1.9 %copy.7 = bf16[128,2048]{1,0:T(8,128)(2,1)} copy(bf16[128,2048]{1,0:T(8,128)(2,1)} %shard_map.55) | data formatting | bytes 1048576
where the time goes:
time: 59.1 us; the launch traced here: 58.9 us
  Pallas kernels  57 us (96%)
  local copies, waits for them, and re-layouts  1.88 us (3%)
    pallas_call x1, Pallas kernels, body(): pl.pallas_call(functools.partial(kernel, owner_count), out_shape=jax.Shap...  57 us
    unnamed x1, local copies, waits for them, and re-layouts  1.88 us

commit v1 on v0

v1 whole, which is shorter than its diff:
```python
import functools

import jax
import jax.numpy as jnp
from jax import lax
from jax.experimental import pallas as pl
from jax.experimental.pallas import tpu as pltpu
from jax.sharding import PartitionSpec as P

SLICES = 4
CHUNKS = 4
STEP = 512
ORDER = (
    "a0c0t1Z1t2N2t3B0v2N3a1c1G0v3O3O2B1P0Q0a2c2",
    "B2G1P1a3c3Q1G2B3P2y2Q2x2E2G3P3Q3y3x3",
    "F2E3x1y1F3E1y0x0F1E0F0",
)
BF16 = jnp.bfloat16
F32 = jnp.float32
MESH = pl.DeviceIdType.MESH


def layout(owner_count, tok_rows):
    groups = owner_count // SLICES
    chunks = CHUNKS
    per = groups // chunks
    seats = 3 * tok_rows // (4 * groups) + tok_rows // (2 * groups)
    unit = 8 if per == 1 else 16
    seats = -(-seats // unit) * unit
    return groups, chunks, per, seats


def stack_rows(blocks):
    return jnp.concatenate([block.astype(F32) for block in blocks], axis=0).astype(BF16)


def flip(a, b, count):
    total, bit = 0, 1
    while bit < count:
        total = total + (a // bit % 2 + b // bit % 2) % 2 * bit
        bit *= 2
    return total


def kernel(
    owner_count,
    ids_hbm,
    gates_hbm,
    tokens_hbm,
    weight_in,
    weight_out,
    out,
    ids_row,
    gates,
    tokens,
    w_in,
    w_out,
    send,
    gathered,
    staged,
    hidden,
    parts,
    diag_a,
    diag_b,
    from_x,
    from_y,
    sums,
    returned,
    w_sem,
    z_send,
    z_recv,
    g_send,
    g_recv,
    r_send,
    r_recv,
    b_send,
    b_recv,
    far_sem,
):
    tok_rows, width = tokens.shape
    groups, chunks, per, seats = layout(owner_count, tok_rows)
    half = width // 2
    halves = (pl.ds(0, half), pl.ds(half, half))
    me = lax.axis_index("ep")
    group = me // SLICES
    lane = me % SLICES
    x_bit, y_bit = lane % 2, lane // 2
    x_lane = y_bit * 2 + (1 - x_bit)
    y_lane = (1 - y_bit) * 2 + x_bit
    d_lane = (1 - y_bit) * 2 + (1 - x_bit)
    x_dev = group * SLICES + x_lane
    y_dev = group * SLICES + y_lane
    inner = (group % 2 + group // 2 % 2) % 2
    chunk_of = [0, 1, 2 + inner, 3 - inner]

    barrier = pltpu.get_barrier_semaphore()
    pl.semaphore_signal(barrier, inc=1, device_id={"ep": x_dev}, device_id_type=MESH)
    pl.semaphore_signal(barrier, inc=1, device_id={"ep": y_dev}, device_id_type=MESH)
    near = groups == 4

    def greet(sem, k):
        other = flip(group, k, groups) * SLICES + lane
        pl.semaphore_signal(sem, inc=1, device_id={"ep": other}, device_id_type=MESH)

    if near:
        greet(barrier, 1)
        pl.when(inner == 1)(lambda: greet(barrier, 3))
        greeted = 3 + inner
    else:
        for k in range(1, groups):
            greet(barrier, k)
        greeted = 2 + groups - 1

    load_ids = pltpu.make_async_copy(ids_hbm, ids_row, w_sem.at[2])
    load_gates = pltpu.make_async_copy(gates_hbm, gates, w_sem.at[3])
    load_tokens = pltpu.make_async_copy(tokens_hbm, tokens, w_sem.at[4])
    load_in = pltpu.make_async_copy(weight_in, w_in, w_sem.at[0])
    load_out = pltpu.make_async_copy(weight_out, w_out, w_sem.at[1])
    for load in (load_ids, load_gates, load_tokens, load_in, load_out):
        load.start()

    lanes_e = -(-groups // 16) * 16
    t0 = lax.broadcasted_iota(jnp.int32, (tok_rows, tok_rows), 0)
    t1 = lax.broadcasted_iota(jnp.int32, (tok_rows, tok_rows), 1)
    load_ids.wait()
    ids = ids_row[...]
    hot = (lax.broadcasted_iota(jnp.int32, (lanes_e, tok_rows), 0) == ids).astype(F32)
    ahead = jnp.dot(hot.astype(BF16), (t0 < t1).astype(F32).astype(BF16), preferred_element_type=F32)
    slot = ids * seats + jnp.sum(hot * ahead, axis=0, keepdims=True).astype(jnp.int32)
    load_gates.wait()
    slot_c = jnp.sum(jnp.where(t0 == t1, slot, 0), axis=1, keepdims=True)
    weight = jnp.sum(jnp.where(t0 == t1, gates[...], 0.0), axis=1, keepdims=True)
    load_tokens.wait()

    def take(target, dst):
        seat = lax.broadcasted_iota(jnp.int32, (seats, tok_rows), 0) + target * seats
        place = (seat == slot).astype(F32).astype(BF16)
        for c in range(0, width, STEP):
            rows = jnp.dot(place, tokens[:, c : c + STEP], preferred_element_type=F32)
            dst[:, c : c + STEP] = rows.astype(BF16)

    def remote(src, dst, s_sem, r_sem, dev):
        return pltpu.make_async_remote_copy(
            src_ref=src,
            dst_ref=dst,
            send_sem=s_sem,
            recv_sem=r_sem,
            device_id={"ep": dev},
            device_id_type=MESH,
        )

    def seat_rows(ref, i):
        return ref.at[pl.ds(i * seats, seats)] if per > 1 else ref

    members = [(p, i) for p in range(chunks) for i in range(per)][1:]
    spread, forward, early, late, z_copies, back = {}, {}, {}, {}, {}, {}

    def take_for(p, i):
        k = chunk_of[p] * per + i
        target = flip(group, k, groups)
        source = send.at[p * per + i]
        landing = seat_rows(gathered.at[chunk_of[p], lane], i)
        take(target, source)
        z_copies[p, i] = [
            remote(
                source.at[:, cols],
                landing.at[:, cols],
                z_send.at[k, h],
                z_recv.at[k, h],
                target * SLICES + lane,
            )
            for h, cols in enumerate(halves)
        ]

    def stage_t(p):
        if per == 1:
            take_for(p, 0)

    def leave(p):
        for i in range(per):
            if (p, i) in z_copies:
                for copy in z_copies[p, i]:
                    copy.start()

    def stage_z(p):
        leave(p)

    def stage_n(p):
        pl.when(inner == 1)(lambda: leave(p))

    def stage_o(p):
        pl.when(inner == 0)(lambda: leave(p))

    def stage_v(p):
        if near and p == 2:
            pl.semaphore_wait(far_sem.at[0], 1)
            pl.when(inner == 1)(lambda: greet(far_sem.at[1], 1))
        if near and p == 3:
            pl.when(inner == 0)(lambda: pl.semaphore_wait(far_sem.at[1], 1))

    def stage_a(p):
        own = [gathered.at[chunk_of[p], lane, :, cols] for cols in halves]

        def arrive(h):
            for i in range(per):
                if (p, i) in z_copies:
                    z_copies[p, i][h].wait_recv()

        spread[p] = [
            remote(own[h], own[h], g_send.at[p, n], g_recv.at[p, n], dev)
            for n, (h, dev) in enumerate(((0, x_dev), (1, y_dev), (1, x_dev), (0, y_dev)))
        ]
        arrive(0)
        spread[p][0].start()
        arrive(1)
        spread[p][1].start()

    def stage_c(p):
        for copy in spread[p][2:]:
            copy.start()

    def stage_b(p):
        first = gathered.at[chunk_of[p], x_lane, :, halves[0]]
        second = gathered.at[chunk_of[p], y_lane, :, halves[1]]
        forward[p] = [
            remote(first, first, g_send.at[p, 4], g_recv.at[p, 4], y_dev),
            remote(second, second, g_send.at[p, 5], g_recv.at[p, 5], x_dev),
        ]
        for arrived, onward in zip(spread[p], forward[p]):
            arrived.wait_recv()
            onward.start()

    rows = per * seats
    tile = STEP

    def stage_g(p):
        for copy in spread[p][2:] + forward[p]:
            copy.wait_recv()
        staged[...] = stack_rows([gathered[chunk_of[p], s] for s in range(SLICES)])
        if p == 0:
            load_in.wait()

        @pl.loop(0, w_in.shape[1] // tile)
        def _(n):
            cols = pl.ds(pl.multiple_of(n * tile, tile), tile)
            value = jnp.dot(staged[...], w_in[:, cols], preferred_element_type=F32)
            hidden[:, cols] = jnp.maximum(value, 0.0).astype(BF16)

        if p == 0:
            load_out.wait()

    def project(p, start):
        @pl.loop(0, half // tile)
        def _(n):
            cols = pl.ds(pl.multiple_of(start + n * tile, tile), tile)
            value = jnp.dot(hidden[...], w_out[:, cols], preferred_element_type=F32)
            for s in range(SLICES):
                parts[p, s, :, cols] = value[s * rows : (s + 1) * rows].astype(BF16)

    def stage_p(p):
        project(p, 0)

    def stage_q(p):
        project(p, half)

    def to(p, n, src, dst, dev):
        return remote(src, dst, r_send.at[p, n], r_recv.at[p, n], dev)

    def stage_y(p):
        early[p, 0] = to(p, 0, parts.at[p, d_lane, :, halves[0]], diag_a.at[p], y_dev)
        early[p, 1] = to(
            p, 1, parts.at[p, y_lane, :, halves[0]], from_y.at[p, :, halves[0]], y_dev
        )
        early[p, 0].start()
        early[p, 1].start()

    def stage_x(p):
        early[p, 2] = to(p, 2, parts.at[p, d_lane, :, halves[1]], diag_b.at[p], x_dev)
        early[p, 3] = to(
            p, 3, parts.at[p, x_lane, :, halves[1]], from_x.at[p, :, halves[1]], x_dev
        )
        early[p, 2].start()
        early[p, 3].start()

    def stage_e(p):
        late[p] = [
            to(p, 4, parts.at[p, x_lane, :, halves[0]], from_x.at[p, :, halves[0]], x_dev),
            to(p, 5, parts.at[p, y_lane, :, halves[1]], from_y.at[p, :, halves[1]], y_dev),
        ]
        early[p, 0].wait_recv()
        parts[p, x_lane, :, :half] = (
            parts[p, x_lane, :, :half].astype(F32) + diag_a[p].astype(F32)
        ).astype(BF16)
        late[p][0].start()
        early[p, 2].wait_recv()
        parts[p, y_lane, :, half:] = (
            parts[p, y_lane, :, half:].astype(F32) + diag_b[p].astype(F32)
        ).astype(BF16)
        late[p][1].start()

    def stage_f(p):
        for h, cols in enumerate((slice(0, half), slice(half, width))):
            for copy in (late[p][h], early[p, 1 + 2 * h]):
                copy.wait_recv()
            sums[p, :, cols] = (
                parts[p, lane, :, cols].astype(F32)
                + from_x[p, :, cols].astype(F32)
                + from_y[p, :, cols].astype(F32)
            ).astype(BF16)
            for i in range(per):
                if (p, i) in z_copies:
                    k = chunk_of[p] * per + i
                    back[p, i, h] = remote(
                        seat_rows(sums.at[p], i).at[:, halves[h]],
                        returned.at[k, :, halves[h]],
                        b_send.at[k, h],
                        b_recv.at[k, h],
                        flip(group, k, groups) * SLICES + lane,
                    )
                    back[p, i, h].start()

    take(group, seat_rows(gathered.at[0, lane], 0))
    if per > 1:
        for p, i in members:
            take_for(p, i)
    pl.semaphore_wait(barrier, greeted)
    if near:

        @pl.when(inner == 1)
        def _():
            greet(far_sem.at[0], 1)
            greet(far_sem.at[0], 3)

    if per > 1:
        leave(0)

    stages = {
        "a": stage_a,
        "c": stage_c,
        "t": stage_t,
        "v": stage_v,
        "Z": stage_z,
        "N": stage_n,
        "O": stage_o,
        "B": stage_b,
        "G": stage_g,
        "P": stage_p,
        "Q": stage_q,
        "y": stage_y,
        "x": stage_x,
        "E": stage_e,
        "F": stage_f,
    }
    order = "".join(ORDER)
    for name, p in zip(order[::2], order[1::2]):
        stages[name](int(p))

    picks = []
    for p in range(chunks):
        for i in range(per):
            target = flip(group, chunk_of[p] * per + i, groups)
            seat = lax.broadcasted_iota(jnp.int32, (tok_rows, seats), 1) + target * seats
            picks.append((seat == slot_c).astype(F32))
    pick = jnp.concatenate(picks, axis=1).astype(BF16)
    for h in range(2):
        for p, i in members:
            back[p, i, h].wait_recv()
        for c in range(h * half, (h + 1) * half, STEP):
            blocks = [sums[0, :seats, c : c + STEP]]
            blocks += [returned[chunk_of[p] * per + i, :, c : c + STEP] for p, i in members]
            picked = jnp.dot(pick, stack_rows(blocks), preferred_element_type=F32)
            out[:, c : c + STEP] = (weight * picked).astype(BF16)

    for p in range(chunks):
        for copy in spread[p] + forward[p] + late[p] + [early[p, n] for n in range(4)]:
            copy.wait_send()
    for p, i in members:
        for h in range(2):
            z_copies[p, i][h].wait_send()
            back[p, i, h].wait_send()


def body(tokens, gates, expert_ids, weight_in, weight_out):
    owner_count = lax.axis_size("ep")
    tok_rows, width = tokens.shape
    groups, chunks, per, seats = layout(owner_count, tok_rows)
    rows = per * seats
    half = width // 2
    hbm = pl.BlockSpec(memory_space=pltpu.HBM)
    dma = pltpu.SemaphoreType.DMA
    return pl.pallas_call(
        functools.partial(kernel, owner_count),
        out_shape=jax.ShapeDtypeStruct((tok_rows, width), BF16),
        in_specs=[hbm] * 5,
        out_specs=pl.BlockSpec(memory_space=pltpu.VMEM),
        scratch_shapes=[
            pltpu.VMEM((1, tok_rows), jnp.int32),
            pltpu.VMEM((1, tok_rows), F32),
            pltpu.VMEM((tok_rows, width), BF16),
            pltpu.VMEM(weight_in.shape, BF16),
            pltpu.VMEM(weight_out.shape, BF16),
            pltpu.VMEM((groups, seats, width), BF16),
            pltpu.VMEM((chunks, SLICES, rows, width), BF16),
            pltpu.VMEM((SLICES * rows, width), BF16),
            pltpu.VMEM((SLICES * rows, weight_in.shape[1]), BF16),
            pltpu.VMEM((chunks, SLICES, rows, width), BF16),
            pltpu.VMEM((chunks, rows, half), BF16),
            pltpu.VMEM((chunks, rows, half), BF16),
            pltpu.VMEM((chunks, rows, width), BF16),
            pltpu.VMEM((chunks, rows, width), BF16),
            pltpu.VMEM((chunks, rows, width), BF16),
            pltpu.VMEM((groups, seats, width), BF16),
            dma((5,)),
            dma((groups, 2)),
            dma((groups, 2)),
            dma((chunks, 6)),
            dma((chunks, 6)),
            dma((chunks, 6)),
            dma((chunks, 6)),
            dma((groups, 2)),
            dma((groups, 2)),
            pltpu.SemaphoreType.REGULAR((2,)),
        ],
        compiler_params=pltpu.CompilerParams(
            collective_id=0, has_side_effects=True, vmem_limit_bytes=48 * 1024 * 1024
        ),
    )(
        *(
            pltpu.with_memory_space_constraint(array, pltpu.HBM)
            for array in (
                expert_ids.reshape(1, tok_rows),
                gates.reshape(1, tok_rows),
                tokens,
                weight_in,
                weight_out,
            )
        )
    )


def solution(mesh):
    in_specs = (
        P(("rep", "ep"), None),
        P(("rep", "ep")),
        P(("rep", "ep"), None),
        P(None, "ep"),
        P("ep", None),
    )
    out_specs = P(("rep", "ep"), None)
    return jax.shard_map(body, mesh=mesh, in_specs=in_specs, out_specs=out_specs, check_vma=False)
```

time: 59.1 us -> 55.6 us (0.941)
  Pallas kernels: 57 us -> 54.7 us
  local copies, waits for them, and re-layouts: 1.88 us -> 0.8 us
    pallas_call x1, Pallas kernels: 57 us -> 54.7 us  [body(): pl.pallas_call(functools.partial(kernel, owner_count), out_shape=jax.Shap...]
    unnamed x1, local copies, waits for them, and re-layouts: 1.88 us -> 0.8 us
where the time goes in v1:
time: 55.6 us; the launch traced here: 55.5 us
  Pallas kernels  54.7 us (98%)
  local copies, waits for them, and re-layouts  0.8 us (1%)
    pallas_call x1, Pallas kernels, body(): pl.pallas_call(functools.partial(kernel, owner_count), out_shape=jax.Shap...  54.7 us

profile of v1, /device:TPU:0, one launch (start us, length us, event | category | flops | bytes accessed | tf_op | source)
XLA Modules:
  0.0 55.5 jit_solution(7659420131689096202)
XLA Ops:
  0.0 54.7 %shard_map.55 = bf16[128,2048]{1,0:T(8,128)(2,1)S(1)} custom-call(s32[1,128]{1,0:T(1,128)} %bitcast.2, f32[1,128]{1,0:T(1,128)} %bitcast.3, bf16[128,2048]{1,0:T(8,128)(2,1)} %tokens_hbm.1, bf16[2048,1024]{1,0:T(8,128)(2,1)} %weight_in.1, bf16[1024,2048]{1,0:T(8,128)(2,1)} %weight_out.1), custom_call_target="tpu_custom_call" | custom-call | tf_op jit(solution)/shard_map/pallas_call | solution.py:391
  54.7 0.8 %copy.7 = bf16[128,2048]{1,0:T(8,128)(2,1)} copy(bf16[128,2048]{1,0:T(8,128)(2,1)S(1)} %shard_map.55) | data formatting | bytes 1048576

commit v2 on v1

--- a/solution.py
+++ b/solution.py
@@ -11,9 +11,9 @@
 CHUNKS = 4
 STEP = 512
 ORDER = (
-    "a0c0t1Z1t2N2t3B0v2N3a1c1G0v3O3O2B1P0Q0a2c2",
-    "B2G1P1a3c3Q1G2B3P2y2Q2x2E2G3P3Q3y3x3",
-    "F2E3x1y1F3E1y0x0F1E0F0",
+    "a0c0t1Z1t2N2C0B0t3u2N3a1c1G0B1C1u3O3P0O2Q0a2c2G1P1C2B2Q1a3c3",
+    "G2x1w1P2B3C3y1Q2x2G3P3E1y3Q3x3H2y2v2E3w3H3w2v3F1I2E2x0y0v1F3",
+    "H1w0v0I3F2H0E0I1R0F0S0I0T0",
 )
 BF16 = jnp.bfloat16
 F32 = jnp.float32
@@ -66,6 +66,7 @@
     from_y,
     sums,
     returned,
+    total,
     w_sem,
     z_send,
     z_recv,
@@ -149,6 +150,9 @@
             device_id_type=MESH,
         )
 
+    def drain(ref, sem):
+        pltpu.make_async_copy(ref, ref, sem).wait()
+
     def seat_rows(ref, i):
         return ref.at[pl.ds(i * seats, seats)] if per > 1 else ref
 
@@ -165,8 +169,8 @@
             remote(
                 source.at[:, cols],
                 landing.at[:, cols],
-                z_send.at[k, h],
-                z_recv.at[k, h],
+                z_send,
+                z_recv.at[k - 1, h],
                 target * SLICES + lane,
             )
             for h, cols in enumerate(halves)
@@ -191,7 +195,7 @@
     def stage_o(p):
         pl.when(inner == 0)(lambda: leave(p))
 
-    def stage_v(p):
+    def stage_u(p):
         if near and p == 2:
             pl.semaphore_wait(far_sem.at[0], 1)
             pl.when(inner == 1)(lambda: greet(far_sem.at[1], 1))
@@ -207,8 +211,14 @@
                     z_copies[p, i][h].wait_recv()
 
         spread[p] = [
-            remote(own[h], own[h], g_send.at[p, n], g_recv.at[p, n], dev)
-            for n, (h, dev) in enumerate(((0, x_dev), (1, y_dev), (1, x_dev), (0, y_dev)))
+            remote(own[h], own[h], g_send, g_recv.at[p, n], dev)
+            for n, h, dev in ((0, 0, x_dev), (1, 1, y_dev), (2, 1, x_dev), (2, 0, y_dev))
+        ]
+        first = gathered.at[chunk_of[p], x_lane, :, halves[0]]
+        second = gathered.at[chunk_of[p], y_lane, :, halves[1]]
+        forward[p] = [
+            remote(first, first, g_send, g_recv.at[p, 2], y_dev),
+            remote(second, second, g_send, g_recv.at[p, 2], x_dev),
         ]
         arrive(0)
         spread[p][0].start()
@@ -220,22 +230,18 @@
             copy.start()
 
     def stage_b(p):
-        first = gathered.at[chunk_of[p], x_lane, :, halves[0]]
-        second = gathered.at[chunk_of[p], y_lane, :, halves[1]]
-        forward[p] = [
-            remote(first, first, g_send.at[p, 4], g_recv.at[p, 4], y_dev),
-            remote(second, second, g_send.at[p, 5], g_recv.at[p, 5], x_dev),
-        ]
-        for arrived, onward in zip(spread[p], forward[p]):
-            arrived.wait_recv()
-            onward.start()
+        spread[p][0].wait_recv()
+        forward[p][0].start()
+
+    def stage_k(p):
+        spread[p][1].wait_recv()
+        forward[p][1].start()
 
     rows = per * seats
     tile = STEP
 
     def stage_g(p):
-        for copy in spread[p][2:] + forward[p]:
-            copy.wait_recv()
+        drain(gathered.at[chunk_of[p], pl.ds(0, 2)], g_recv.at[p, 2])
         staged[...] = stack_rows([gathered[chunk_of[p], s] for s in range(SLICES)])
         if p == 0:
             load_in.wait()
@@ -264,60 +270,107 @@
         project(p, half)
 
     def to(p, n, src, dst, dev):
-        return remote(src, dst, r_send.at[p, n], r_recv.at[p, n], dev)
+        return remote(src, dst, r_send, r_recv.at[p, n], dev)
 
     def stage_y(p):
         early[p, 0] = to(p, 0, parts.at[p, d_lane, :, halves[0]], diag_a.at[p], y_dev)
+        early[p, 0].start()
+
+    def stage_w(p):
         early[p, 1] = to(
-            p, 1, parts.at[p, y_lane, :, halves[0]], from_y.at[p, :, halves[0]], y_dev
+            p, 2, parts.at[p, y_lane, :, halves[0]], from_y.at[p, :, halves[0]], y_dev
         )
-        early[p, 0].start()
         early[p, 1].start()
 
     def stage_x(p):
-        early[p, 2] = to(p, 2, parts.at[p, d_lane, :, halves[1]], diag_b.at[p], x_dev)
+        early[p, 2] = to(p, 1, parts.at[p, d_lane, :, halves[1]], diag_b.at[p], x_dev)
+        early[p, 2].start()
+
+    def stage_v(p):
         early[p, 3] = to(
             p, 3, parts.at[p, x_lane, :, halves[1]], from_x.at[p, :, halves[1]], x_dev
         )
-        early[p, 2].start()
         early[p, 3].start()
 
     def stage_e(p):
-        late[p] = [
-            to(p, 4, parts.at[p, x_lane, :, halves[0]], from_x.at[p, :, halves[0]], x_dev),
-            to(p, 5, parts.at[p, y_lane, :, halves[1]], from_y.at[p, :, halves[1]], y_dev),
-        ]
+        late[p, 0] = to(p, 2, parts.at[p, x_lane, :, halves[0]], from_x.at[p, :, halves[0]], x_dev)
         early[p, 0].wait_recv()
         parts[p, x_lane, :, :half] = (
             parts[p, x_lane, :, :half].astype(F32) + diag_a[p].astype(F32)
         ).astype(BF16)
-        late[p][0].start()
+        late[p, 0].start()
+
+    def stage_h(p):
+        late[p, 1] = to(p, 3, parts.at[p, y_lane, :, halves[1]], from_y.at[p, :, halves[1]], y_dev)
         early[p, 2].wait_recv()
         parts[p, y_lane, :, half:] = (
             parts[p, y_lane, :, half:].astype(F32) + diag_b[p].astype(F32)
         ).astype(BF16)
-        late[p][1].start()
+        late[p, 1].start()
+
+    def finish(p, h):
+        cols = slice(h * half, (h + 1) * half)
+        drain(from_x.at[p], r_recv.at[p, 2 + h])
+        sums[p, :, cols] = (
+            parts[p, lane, :, cols].astype(F32)
+            + from_x[p, :, cols].astype(F32)
+            + from_y[p, :, cols].astype(F32)
+        ).astype(BF16)
+        for i in range(per):
+            if (p, i) in z_copies:
+                k = chunk_of[p] * per + i
+                back[p, i, h] = remote(
+                    seat_rows(sums.at[p], i).at[:, halves[h]],
+                    returned.at[k, :, halves[h]],
+                    b_send,
+                    b_recv.at[0 if p > 0 else 1 + h],
+                    flip(group, k, groups) * SLICES + lane,
+                )
+                back[p, i, h].start()
 
     def stage_f(p):
-        for h, cols in enumerate((slice(0, half), slice(half, width))):
-            for copy in (late[p][h], early[p, 1 + 2 * h]):
-                copy.wait_recv()
-            sums[p, :, cols] = (
-                parts[p, lane, :, cols].astype(F32)
-                + from_x[p, :, cols].astype(F32)
-                + from_y[p, :, cols].astype(F32)
-            ).astype(BF16)
-            for i in range(per):
-                if (p, i) in z_copies:
-                    k = chunk_of[p] * per + i
-                    back[p, i, h] = remote(
-                        seat_rows(sums.at[p], i).at[:, halves[h]],
-                        returned.at[k, :, halves[h]],
-                        b_send.at[k, h],
-                        b_recv.at[k, h],
-                        flip(group, k, groups) * SLICES + lane,
-                    )
-                    back[p, i, h].start()
+        finish(p, 0)
+
+    def stage_i(p):
+        finish(p, 1)
+
+    def picks_of(wanted):
+        picks = []
+        for p, i in wanted:
+            target = flip(group, chunk_of[p] * per + i, groups)
+            seat = lax.broadcasted_iota(jnp.int32, (tok_rows, seats), 1) + target * seats
+            picks.append((seat == slot_c).astype(F32))
+        return jnp.concatenate(picks, axis=1).astype(BF16)
+
+    def gather(wanted, h, c):
+        blocks = []
+        for q, i in wanted:
+            if (q, i) == (0, 0):
+                blocks.append(sums[0, :seats, c : c + STEP])
+            else:
+                blocks.append(returned[chunk_of[q] * per + i, :, c : c + STEP])
+        return jnp.dot(picks_of(wanted), stack_rows(blocks), preferred_element_type=F32)
+
+    def stage_r(p):
+        wanted = [(q, i) for q, i in members if q > 0]
+        drain(returned.at[pl.ds(0, len(wanted))], b_recv.at[0])
+        for h in range(2):
+            for c in range(h * half, (h + 1) * half, STEP):
+                total[:, c : c + STEP] = gather(wanted, h, c)
+
+    def store(h):
+        if per > 1:
+            drain(returned.at[pl.ds(0, per - 1), :, halves[h]], b_recv.at[1 + h])
+        wanted = [(0, i) for i in range(per)]
+        for c in range(h * half, (h + 1) * half, STEP):
+            picked = total[:, c : c + STEP] + gather(wanted, h, c)
+            out[:, c : c + STEP] = (weight * picked).astype(BF16)
+
+    def stage_s(p):
+        store(0)
+
+    def stage_j(p):
+        store(1)
 
     take(group, seat_rows(gathered.at[0, lane], 0))
     if per > 1:
@@ -338,46 +391,35 @@
         "a": stage_a,
         "c": stage_c,
         "t": stage_t,
-        "v": stage_v,
+        "u": stage_u,
         "Z": stage_z,
         "N": stage_n,
         "O": stage_o,
         "B": stage_b,
+        "C": stage_k,
         "G": stage_g,
         "P": stage_p,
         "Q": stage_q,
         "y": stage_y,
+        "w": stage_w,
         "x": stage_x,
+        "v": stage_v,
         "E": stage_e,
+        "H": stage_h,
         "F": stage_f,
+        "I": stage_i,
+        "R": stage_r,
+        "S": stage_s,
+        "T": stage_j,
     }
     order = "".join(ORDER)
     for name, p in zip(order[::2], order[1::2]):
         stages[name](int(p))
 
-    picks = []
-    for p in range(chunks):
-        for i in range(per):
-            target = flip(group, chunk_of[p] * per + i, groups)
-            seat = lax.broadcasted_iota(jnp.int32, (tok_rows, seats), 1) + target * seats
-            picks.append((seat == slot_c).astype(F32))
-    pick = jnp.concatenate(picks, axis=1).astype(BF16)
-    for h in range(2):
-        for p, i in members:
-            back[p, i, h].wait_recv()
-        for c in range(h * half, (h + 1) * half, STEP):
-            blocks = [sums[0, :seats, c : c + STEP]]
-            blocks += [returned[chunk_of[p] * per + i, :, c : c + STEP] for p, i in members]
-            picked = jnp.dot(pick, stack_rows(blocks), preferred_element_type=F32)
-            out[:, c : c + STEP] = (weight * picked).astype(BF16)
-
-    for p in range(chunks):
-        for copy in spread[p] + forward[p] + late[p] + [early[p, n] for n in range(4)]:
-            copy.wait_send()
-    for p, i in members:
-        for h in range(2):
-            z_copies[p, i][h].wait_send()
-            back[p, i, h].wait_send()
+    drain(send.at[pl.ds(0, len(members))], z_send)
+    drain(parts.at[pl.ds(0, 3)], g_send)
+    drain(parts.at[pl.ds(0, 3)], r_send)
+    drain(returned.at[pl.ds(0, len(members))], b_send)
 
 
 def body(tokens, gates, expert_ids, weight_in, weight_out):
@@ -410,15 +452,16 @@
             pltpu.VMEM((chunks, rows, width), BF16),
             pltpu.VMEM((chunks, rows, width), BF16),
             pltpu.VMEM((groups, seats, width), BF16),
+            pltpu.VMEM((tok_rows, width), F32),
             dma((5,)),
-            dma((groups, 2)),
-            dma((groups, 2)),
-            dma((chunks, 6)),
-            dma((chunks, 6)),
-            dma((chunks, 6)),
-            dma((chunks, 6)),
-            dma((groups, 2)),
-            dma((groups, 2)),
+            dma,
+            dma((groups - 1, 2)),
+            dma,
+            dma((chunks, 3)),
+            dma,
+            dma((chunks, 4)),
+            dma,
+            dma((3,)),
             pltpu.SemaphoreType.REGULAR((2,)),
         ],
         compiler_params=pltpu.CompilerParams(

time: 55.6 us -> 52.5 us (0.944)
  Pallas kernels: 54.7 us -> 51.5 us
    pallas_call x1, Pallas kernels: 54.7 us -> 51.5 us  [body(): pl.pallas_call(functools.partial(kernel, owner_count), out_shape=jax.Shap...]
where the time goes in v2:
time: 52.5 us; the launch traced here: 52.3 us
  Pallas kernels  51.5 us (98%)
  local copies, waits for them, and re-layouts  0.8 us (2%)
    pallas_call x1, Pallas kernels, body(): pl.pallas_call(functools.partial(kernel, owner_count), out_shape=jax.Shap...  51.5 us

profile of v2, /device:TPU:0, one launch (start us, length us, event | category | flops | bytes accessed | tf_op | source)
XLA Modules:
  0.0 52.3 jit_solution(16469121254964526146)
XLA Ops:
  0.0 51.5 %shard_map.55 = bf16[128,2048]{1,0:T(8,128)(2,1)S(1)} custom-call(s32[1,128]{1,0:T(1,128)} %bitcast.2, f32[1,128]{1,0:T(1,128)} %bitcast.3, bf16[128,2048]{1,0:T(8,128)(2,1)} %tokens_hbm.1, bf16[2048,1024]{1,0:T(8,128)(2,1)} %weight_in.1, bf16[1024,2048]{1,0:T(8,128)(2,1)} %weight_out.1), custom_call_target="tpu_custom_call" | custom-call | tf_op jit(solution)/shard_map/pallas_call | solution.py:433
  51.5 0.8 %copy.7 = bf16[128,2048]{1,0:T(8,128)(2,1)} copy(bf16[128,2048]{1,0:T(8,128)(2,1)S(1)} %shard_map.55) | data formatting | bytes 1048576

commit v3 on v1

v3 whole, which is shorter than its diff:
```python
import functools

import jax
import jax.numpy as jnp
from jax import lax
from jax.experimental import pallas as pl
from jax.experimental.pallas import tpu as pltpu
from jax.sharding import PartitionSpec as P

SLICES = 4
CHUNKS = 4
STEP = 512
ORDER = (
    "a0c0t1Z1t2N2C0B0t3u2N3a1c1G0B1C1u3O3P0O2Q0a2c2G1P1C2B2Q1a3c3",
    "G2x1w1P2C3B3y1Q2x2G3P3E1y3Q3x3H2y2v2E3w3H3w2v3F1I2E2x0y0v1F3",
    "H1v0I3F2H0w0E0I1R3F0I0S2T1",
)
OTHER = ORDER
BF16 = jnp.bfloat16
F32 = jnp.float32
MESH = pl.DeviceIdType.MESH


def layout(owner_count, tok_rows):
    groups = owner_count // SLICES
    chunks = CHUNKS
    per = groups // chunks
    seats = 3 * tok_rows // (4 * groups) + tok_rows // (2 * groups)
    unit = 8 if per == 1 else 16
    seats = -(-seats // unit) * unit
    return groups, chunks, per, seats


def stack_rows(blocks):
    return jnp.concatenate([block.astype(F32) for block in blocks], axis=0).astype(BF16)


def flip(a, b, count):
    total, bit = 0, 1
    while bit < count:
        total = total + (a // bit % 2 + b // bit % 2) % 2 * bit
        bit *= 2
    return total


def kernel(
    owner_count,
    ids_hbm,
    gates_hbm,
    tokens_hbm,
    weight_in,
    weight_out,
    out,
    ids_row,
    gates,
    tokens,
    w_in,
    w_out,
    send,
    gathered,
    staged,
    hidden,
    parts,
    diag_a,
    diag_b,
    from_x,
    from_y,
    sums,
    returned,
    total,
    w_sem,
    z_send,
    z_recv,
    g_send,
    g_recv,
    r_send,
    r_recv,
    b_send,
    b_recv,
    far_sem,
):
    tok_rows, width = tokens.shape
    groups, chunks, per, seats = layout(owner_count, tok_rows)
    half = width // 2
    halves = (pl.ds(0, half), pl.ds(half, half))
    me = lax.axis_index("ep")
    group = me // SLICES
    lane = me % SLICES
    x_bit, y_bit = lane % 2, lane // 2
    x_lane = y_bit * 2 + (1 - x_bit)
    y_lane = (1 - y_bit) * 2 + x_bit
    d_lane = (1 - y_bit) * 2 + (1 - x_bit)
    x_dev = group * SLICES + x_lane
    y_dev = group * SLICES + y_lane
    inner = (group % 2 + group // 2 % 2) % 2
    chunk_of = [0, 1, 2 + inner, 3 - inner]

    barrier = pltpu.get_barrier_semaphore()
    pl.semaphore_signal(barrier, inc=1, device_id={"ep": x_dev}, device_id_type=MESH)
    pl.semaphore_signal(barrier, inc=1, device_id={"ep": y_dev}, device_id_type=MESH)
    near = groups == 4

    def greet(sem, k):
        other = flip(group, k, groups) * SLICES + lane
        pl.semaphore_signal(sem, inc=1, device_id={"ep": other}, device_id_type=MESH)

    if near:
        greet(barrier, 1)
        pl.when(inner == 1)(lambda: greet(barrier, 3))
        greeted = 3 + inner
    else:
        for k in range(1, groups):
            greet(barrier, k)
        greeted = 2 + groups - 1

    load_ids = pltpu.make_async_copy(ids_hbm, ids_row, w_sem.at[2])
    load_gates = pltpu.make_async_copy(gates_hbm, gates, w_sem.at[3])
    load_tokens = pltpu.make_async_copy(tokens_hbm, tokens, w_sem.at[4])
    load_in = pltpu.make_async_copy(weight_in, w_in, w_sem.at[0])
    load_out = pltpu.make_async_copy(weight_out, w_out, w_sem.at[1])
    for load in (load_ids, load_gates, load_tokens, load_in, load_out):
        load.start()

    lanes_e = -(-groups // 16) * 16
    t0 = lax.broadcasted_iota(jnp.int32, (tok_rows, tok_rows), 0)
    t1 = lax.broadcasted_iota(jnp.int32, (tok_rows, tok_rows), 1)
    load_ids.wait()
    ids = ids_row[...]
    hot = (lax.broadcasted_iota(jnp.int32, (lanes_e, tok_rows), 0) == ids).astype(F32)
    ahead = jnp.dot(hot.astype(BF16), (t0 < t1).astype(F32).astype(BF16), preferred_element_type=F32)
    slot = ids * seats + jnp.sum(hot * ahead, axis=0, keepdims=True).astype(jnp.int32)
    load_gates.wait()
    slot_c = jnp.sum(jnp.where(t0 == t1, slot, 0), axis=1, keepdims=True)
    weight = jnp.sum(jnp.where(t0 == t1, gates[...], 0.0), axis=1, keepdims=True)
    load_tokens.wait()

    def take(target, dst):
        seat = lax.broadcasted_iota(jnp.int32, (seats, tok_rows), 0) + target * seats
        place = (seat == slot).astype(F32).astype(BF16)
        for c in range(0, width, STEP):
            rows = jnp.dot(place, tokens[:, c : c + STEP], preferred_element_type=F32)
            dst[:, c : c + STEP] = rows.astype(BF16)

    def remote(src, dst, s_sem, r_sem, dev):
        return pltpu.make_async_remote_copy(
            src_ref=src,
            dst_ref=dst,
            send_sem=s_sem,
            recv_sem=r_sem,
            device_id={"ep": dev},
            device_id_type=MESH,
        )

    def drain(ref, sem):
        pltpu.make_async_copy(ref, ref, sem).wait()

    def seat_rows(ref, i):
        return ref.at[pl.ds(i * seats, seats)] if per > 1 else ref

    def run(order):
        members = [(p, i) for p in range(chunks) for i in range(per)][1:]
        spread, forward, early, late, z_copies, back = {}, {}, {}, {}, {}, {}

        def take_for(p, i):
            k = chunk_of[p] * per + i
            target = flip(group, k, groups)
            source = send.at[p * per + i]
            landing = seat_rows(gathered.at[chunk_of[p], lane], i)
            take(target, source)
            z_copies[p, i] = [
                remote(
                    source.at[:, cols],
                    landing.at[:, cols],
                    z_send,
                    z_recv.at[k - 1, h],
                    target * SLICES + lane,
                )
                for h, cols in enumerate(halves)
            ]

        def stage_t(p):
            if per == 1:
                take_for(p, 0)

        def leave(p):
            for i in range(per):
                if (p, i) in z_copies:
                    for copy in z_copies[p, i]:
                        copy.start()

        def stage_z(p):
            leave(p)

        def stage_n(p):
            pl.when(inner == 1)(lambda: leave(p))

        def stage_o(p):
            pl.when(inner == 0)(lambda: leave(p))

        def stage_u(p):
            if near and p == 2:
                pl.semaphore_wait(far_sem.at[0], 1)
                pl.when(inner == 1)(lambda: greet(far_sem.at[1], 1))
            if near and p == 3:
                pl.when(inner == 0)(lambda: pl.semaphore_wait(far_sem.at[1], 1))

        def stage_a(p):
            own = [gathered.at[chunk_of[p], lane, :, cols] for cols in halves]

            def arrive(h):
                for i in range(per):
                    if (p, i) in z_copies:
                        z_copies[p, i][h].wait_recv()

            spread[p] = [
                remote(own[h], own[h], g_send, g_recv.at[p, n], dev)
                for n, h, dev in ((0, 0, x_dev), (1, 1, y_dev), (2, 1, x_dev), (2, 0, y_dev))
            ]
            first = gathered.at[chunk_of[p], x_lane, :, halves[0]]
            second = gathered.at[chunk_of[p], y_lane, :, halves[1]]
            forward[p] = [
                remote(first, first, g_send, g_recv.at[p, 2], y_dev),
                remote(second, second, g_send, g_recv.at[p, 2], x_dev),
            ]
            arrive(0)
            spread[p][0].start()
            arrive(1)
            spread[p][1].start()

        def stage_c(p):
            for copy in spread[p][2:]:
                copy.start()

        def stage_b(p):
            spread[p][0].wait_recv()
            forward[p][0].start()

        def stage_k(p):
            spread[p][1].wait_recv()
            forward[p][1].start()

        rows = per * seats
        tile = STEP

        def stage_g(p):
            drain(gathered.at[chunk_of[p], pl.ds(0, 2)], g_recv.at[p, 2])
            staged[...] = stack_rows([gathered[chunk_of[p], s] for s in range(SLICES)])
            if p == 0:
                load_in.wait()

            @pl.loop(0, w_in.shape[1] // tile)
            def _(n):
                cols = pl.ds(pl.multiple_of(n * tile, tile), tile)
                value = jnp.dot(staged[...], w_in[:, cols], preferred_element_type=F32)
                hidden[:, cols] = jnp.maximum(value, 0.0).astype(BF16)

            if p == 0:
                load_out.wait()

        def project(p, start):
            @pl.loop(0, half // tile)
            def _(n):
                cols = pl.ds(pl.multiple_of(start + n * tile, tile), tile)
                value = jnp.dot(hidden[...], w_out[:, cols], preferred_element_type=F32)
                for s in range(SLICES):
                    parts[p, s, :, cols] = value[s * rows : (s + 1) * rows].astype(BF16)

        def stage_p(p):
            project(p, 0)

        def stage_q(p):
            project(p, half)

        def to(p, n, src, dst, dev):
            return remote(src, dst, r_send, r_recv.at[p, n], dev)

        def stage_y(p):
            early[p, 0] = to(p, 0, parts.at[p, d_lane, :, halves[0]], diag_a.at[p], y_dev)
            early[p, 0].start()

        def stage_w(p):
            early[p, 1] = to(
                p, 2, parts.at[p, y_lane, :, halves[0]], from_y.at[p, :, halves[0]], y_dev
            )
            early[p, 1].start()

        def stage_x(p):
            early[p, 2] = to(p, 1, parts.at[p, d_lane, :, halves[1]], diag_b.at[p], x_dev)
            early[p, 2].start()

        def stage_v(p):
            early[p, 3] = to(
                p, 3, parts.at[p, x_lane, :, halves[1]], from_x.at[p, :, halves[1]], x_dev
            )
            early[p, 3].start()

        def stage_e(p):
            late[p, 0] = to(p, 2, parts.at[p, x_lane, :, halves[0]], from_x.at[p, :, halves[0]], x_dev)
            early[p, 0].wait_recv()
            parts[p, x_lane, :, :half] = (
                parts[p, x_lane, :, :half].astype(F32) + diag_a[p].astype(F32)
            ).astype(BF16)
            late[p, 0].start()

        def stage_h(p):
            late[p, 1] = to(p, 3, parts.at[p, y_lane, :, halves[1]], from_y.at[p, :, halves[1]], y_dev)
            early[p, 2].wait_recv()
            parts[p, y_lane, :, half:] = (
                parts[p, y_lane, :, half:].astype(F32) + diag_b[p].astype(F32)
            ).astype(BF16)
            late[p, 1].start()

        def finish(p, h):
            cols = slice(h * half, (h + 1) * half)
            drain(from_x.at[p], r_recv.at[p, 2 + h])
            sums[p, :, cols] = (
                parts[p, lane, :, cols].astype(F32)
                + from_x[p, :, cols].astype(F32)
                + from_y[p, :, cols].astype(F32)
            ).astype(BF16)
            for i in range(per):
                if (p, i) in z_copies:
                    k = chunk_of[p] * per + i
                    back[p, i, h] = remote(
                        seat_rows(sums.at[p], i).at[:, halves[h]],
                        returned.at[k, :, halves[h]],
                        b_send,
                        b_recv.at[chunk_of[p]],
                        flip(group, k, groups) * SLICES + lane,
                    )
                    back[p, i, h].start()

        def stage_f(p):
            finish(p, 0)

        def stage_i(p):
            finish(p, 1)

        def picks_of(wanted):
            picks = []
            for p, i in wanted:
                target = flip(group, chunk_of[p] * per + i, groups)
                seat = lax.broadcasted_iota(jnp.int32, (tok_rows, seats), 1) + target * seats
                picks.append((seat == slot_c).astype(F32))
            return jnp.concatenate(picks, axis=1).astype(BF16)

        def gather(wanted, c):
            blocks = []
            for q, i in wanted:
                if (q, i) == (0, 0):
                    blocks.append(sums[0, :seats, c : c + STEP])
                else:
                    blocks.append(returned[chunk_of[q] * per + i, :, c : c + STEP])
            return jnp.dot(picks_of(wanted), stack_rows(blocks), preferred_element_type=F32)

        def returns(p):
            count = per - 1 if p == 0 else per
            if count:
                drain(returned.at[pl.ds(0, count)], b_recv.at[chunk_of[p]])
            return [(p, i) for i in range(per)]

        def stage_r(p):
            wanted = returns(p)
            for c in range(0, width, STEP):
                total[:, c : c + STEP] = gather(wanted, c)

        def stage_s(p):
            wanted = returns(0) + returns(p)
            for c in range(0, width, STEP):
                total[:, c : c + STEP] += gather(wanted, c)

        def stage_j(p):
            wanted = returns(p)
            for c in range(0, width, STEP):
                picked = total[:, c : c + STEP] + gather(wanted, c)
                out[:, c : c + STEP] = (weight * picked).astype(BF16)

        take(group, seat_rows(gathered.at[0, lane], 0))
        if per > 1:
            for p, i in members:
                take_for(p, i)
        pl.semaphore_wait(barrier, greeted)
        if near:

            @pl.when(inner == 1)
            def _():
                greet(far_sem.at[0], 1)
                greet(far_sem.at[0], 3)

        if per > 1:
            leave(0)

        stages = {
            "a": stage_a,
            "c": stage_c,
            "t": stage_t,
            "u": stage_u,
            "Z": stage_z,
            "N": stage_n,
            "O": stage_o,
            "B": stage_b,
            "C": stage_k,
            "G": stage_g,
            "P": stage_p,
            "Q": stage_q,
            "y": stage_y,
            "w": stage_w,
            "x": stage_x,
            "v": stage_v,
            "E": stage_e,
            "H": stage_h,
            "F": stage_f,
            "I": stage_i,
            "R": stage_r,
            "S": stage_s,
            "T": stage_j,
        }
        for name, p in zip(order[::2], order[1::2]):
            stages[name](int(p))

        drain(send.at[pl.ds(0, len(members))], z_send)
        drain(parts.at[pl.ds(0, 3)], g_send)
        drain(parts.at[pl.ds(0, 3)], r_send)
        drain(returned.at[pl.ds(0, len(members))], b_send)

    if ORDER == OTHER:
        run("".join(ORDER))
    else:
        core = lax.axis_index("rep")
        pl.when(core == 0)(lambda: run("".join(ORDER)))
        pl.when(core != 0)(lambda: run("".join(OTHER)))


def body(tokens, gates, expert_ids, weight_in, weight_out):
    owner_count = lax.axis_size("ep")
    tok_rows, width = tokens.shape
    groups, chunks, per, seats = layout(owner_count, tok_rows)
    rows = per * seats
    half = width // 2
    hbm = pl.BlockSpec(memory_space=pltpu.HBM)
    dma = pltpu.SemaphoreType.DMA
    return pl.pallas_call(
        functools.partial(kernel, owner_count),
        out_shape=jax.ShapeDtypeStruct((tok_rows, width), BF16),
        in_specs=[hbm] * 5,
        out_specs=pl.BlockSpec(memory_space=pltpu.VMEM),
        scratch_shapes=[
            pltpu.VMEM((1, tok_rows), jnp.int32),
            pltpu.VMEM((1, tok_rows), F32),
            pltpu.VMEM((tok_rows, width), BF16),
            pltpu.VMEM(weight_in.shape, BF16),
            pltpu.VMEM(weight_out.shape, BF16),
            pltpu.VMEM((groups, seats, width), BF16),
            pltpu.VMEM((chunks, SLICES, rows, width), BF16),
            pltpu.VMEM((SLICES * rows, width), BF16),
            pltpu.VMEM((SLICES * rows, weight_in.shape[1]), BF16),
            pltpu.VMEM((chunks, SLICES, rows, width), BF16),
            pltpu.VMEM((chunks, rows, half), BF16),
            pltpu.VMEM((chunks, rows, half), BF16),
            pltpu.VMEM((chunks, rows, width), BF16),
            pltpu.VMEM((chunks, rows, width), BF16),
            pltpu.VMEM((chunks, rows, width), BF16),
            pltpu.VMEM((groups, seats, width), BF16),
            pltpu.VMEM((tok_rows, width), F32),
            dma((5,)),
            dma,
            dma((groups - 1, 2)),
            dma,
            dma((chunks, 3)),
            dma,
            dma((chunks, 4)),
            dma,
            dma((chunks,)),
            pltpu.SemaphoreType.REGULAR((2,)),
        ],
        compiler_params=pltpu.CompilerParams(
            collective_id=0, has_side_effects=True, vmem_limit_bytes=48 * 1024 * 1024
        ),
    )(
        *(
            pltpu.with_memory_space_constraint(array, pltpu.HBM)
            for array in (
                expert_ids.reshape(1, tok_rows),
                gates.reshape(1, tok_rows),
                tokens,
                weight_in,
                weight_out,
            )
        )
    )


def solution(mesh):
    in_specs = (
        P(("rep", "ep"), None),
        P(("rep", "ep")),
        P(("rep", "ep"), None),
        P(None, "ep"),
        P("ep", None),
    )
    out_specs = P(("rep", "ep"), None)
    return jax.shard_map(body, mesh=mesh, in_specs=in_specs, out_specs=out_specs, check_vma=False)
```

time: 55.6 us -> 52.2 us (0.939)
  Pallas kernels: 54.7 us -> 51.2 us
    pallas_call x1, Pallas kernels: 54.7 us -> 51.2 us  [body(): pl.pallas_call(functools.partial(kernel, owner_count), out_shape=jax.Shap...]
where the time goes in v3:
time: 52.2 us; the launch traced here: 52 us
  Pallas kernels  51.2 us (98%)
  local copies, waits for them, and re-layouts  0.8 us (2%)
    pallas_call x1, Pallas kernels, body(): pl.pallas_call(functools.partial(kernel, owner_count), out_shape=jax.Shap...  51.2 us

profile of v3, /device:TPU:0, one launch (start us, length us, event | category | flops | bytes accessed | tf_op | source)
XLA Modules:
  0.0 52.0 jit_solution(15629886089673890493)
XLA Ops:
  0.0 51.2 %shard_map.55 = bf16[128,2048]{1,0:T(8,128)(2,1)S(1)} custom-call(s32[1,128]{1,0:T(1,128)} %bitcast.2, f32[1,128]{1,0:T(1,128)} %bitcast.3, bf16[128,2048]{1,0:T(8,128)(2,1)} %tokens_hbm.1, bf16[2048,1024]{1,0:T(8,128)(2,1)} %weight_in.1, bf16[1024,2048]{1,0:T(8,128)(2,1)} %weight_out.1), custom_call_target="tpu_custom_call" | custom-call | tf_op jit(solution)/shard_map/pallas_call | solution.py:442
  51.3 0.8 %copy.7 = bf16[128,2048]{1,0:T(8,128)(2,1)} copy(bf16[128,2048]{1,0:T(8,128)(2,1)S(1)} %shard_map.55) | data formatting | bytes 1048576

commit v4 on v3

--- a/solution.py
+++ b/solution.py
@@ -11,8 +11,8 @@
 CHUNKS = 4
 STEP = 512
 ORDER = (
-    "a0c0t1Z1t2N2C0B0t3u2N3a1c1G0B1C1u3O3P0O2Q0a2c2G1P1C2B2Q1a3c3",
-    "G2x1w1P2C3B3y1Q2x2G3P3E1y3Q3x3H2y2v2E3w3H3w2v3F1I2E2x0y0v1F3",
+    "a0c0t1Z1t2N2C0B0t3u2N3a1c1G0B1C1u3O3P0O2a2Q0c2G1P1C2B2Q1a3c3",
+    "G2x1w1P2C3B3y1Q2x2G3P3E1v2y3Q3x3H2y2E3w3H3w2v3F1I2E2x0y0v1F3",
     "H1v0I3F2H0w0E0I1R3F0I0S2T1",
 )
 OTHER = ORDER
@@ -344,35 +344,44 @@
                 picks.append((seat == slot_c).astype(F32))
             return jnp.concatenate(picks, axis=1).astype(BF16)
 
-        def gather(wanted, c):
+        def gather(pick, wanted, c):
             blocks = []
             for q, i in wanted:
                 if (q, i) == (0, 0):
                     blocks.append(sums[0, :seats, c : c + STEP])
                 else:
                     blocks.append(returned[chunk_of[q] * per + i, :, c : c + STEP])
-            return jnp.dot(picks_of(wanted), stack_rows(blocks), preferred_element_type=F32)
+            return jnp.dot(pick, stack_rows(blocks), preferred_element_type=F32)
 
         def returns(p):
             count = per - 1 if p == 0 else per
             if count:
                 drain(returned.at[pl.ds(0, count)], b_recv.at[chunk_of[p]])
+
+        def rows_of(p):
             return [(p, i) for i in range(per)]
 
         def stage_r(p):
-            wanted = returns(p)
+            wanted = rows_of(p)
+            pick = picks_of(wanted)
+            returns(p)
             for c in range(0, width, STEP):
-                total[:, c : c + STEP] = gather(wanted, c)
+                total[:, c : c + STEP] = gather(pick, wanted, c)
 
         def stage_s(p):
-            wanted = returns(0) + returns(p)
+            wanted = rows_of(0) + rows_of(p)
+            pick = picks_of(wanted)
+            returns(0)
+            returns(p)
             for c in range(0, width, STEP):
-                total[:, c : c + STEP] += gather(wanted, c)
+                total[:, c : c + STEP] += gather(pick, wanted, c)
 
         def stage_j(p):
-            wanted = returns(p)
+            wanted = rows_of(p)
+            pick = picks_of(wanted)
+            returns(p)
             for c in range(0, width, STEP):
-                picked = total[:, c : c + STEP] + gather(wanted, c)
+                picked = total[:, c : c + STEP] + gather(pick, wanted, c)
                 out[:, c : c + STEP] = (weight * picked).astype(BF16)
 
         take(group, seat_rows(gathered.at[0, lane], 0))

time: 52.2 us -> 52.1 us (level)
  no operation moved by 1% of the time
where the time goes in v4:
time: 52.1 us; the launch traced here: 52 us
  Pallas kernels  51.2 us (98%)
  local copies, waits for them, and re-layouts  0.8 us (2%)
    pallas_call x1, Pallas kernels, body(): pl.pallas_call(functools.partial(kernel, owner_count), out_shape=jax.Shap...  51.2 us

profile of v4, /device:TPU:0, one launch (start us, length us, event | category | flops | bytes accessed | tf_op | source)
XLA Modules:
  0.0 52.0 jit_solution(13965471737761028599)
XLA Ops:
  0.0 51.2 %shard_map.55 = bf16[128,2048]{1,0:T(8,128)(2,1)S(1)} custom-call(s32[1,128]{1,0:T(1,128)} %bitcast.2, f32[1,128]{1,0:T(1,128)} %bitcast.3, bf16[128,2048]{1,0:T(8,128)(2,1)} %tokens_hbm.1, bf16[2048,1024]{1,0:T(8,128)(2,1)} %weight_in.1, bf16[1024,2048]{1,0:T(8,128)(2,1)} %weight_out.1), custom_call_target="tpu_custom_call" | custom-call | tf_op jit(solution)/shard_map/pallas_call | solution.py:451
  51.2 0.8 %copy.7 = bf16[128,2048]{1,0:T(8,128)(2,1)} copy(bf16[128,2048]{1,0:T(8,128)(2,1)S(1)} %shard_map.55) | data formatting | bytes 1048576
